TPU v7x, 128 devices: a whole 4x4x4 slice. The times are simulated.
128 devices in a mesh: fsdp: 32 (over z_hi, y, x), tp: 4 (over z_lo, core).
Axes of the slice: x: 4, y: 4, z: 4 (z_hi: 2, z_lo: 2; z = z_hi * 2 + z_lo), core: 2. Of those that a mesh axis runs over, the one named last changes fastest.
Arguments:
- weights: bfloat16 [8192, 16384], P('fsdp', 'tp')
- owner_map: int32 [128, 256], P(('fsdp', 'tp')), may hold values from 0 to 127, as said below
Outputs:
- served_tiles: bfloat16 [32768, 32, 128], P(('fsdp', 'tp'))
- served_scales: float32 [32768, 128], P(('fsdp', 'tp'))
Inputs may be any that keep to these rules, and one draw needn't show every extreme that they name: `owner_map`: each source device's row names every destination exactly 2 times.
All inputs are finite; a program needn't handle non-finite values. Where the computation divides by a largest or mean magnitude, that divisor is 1e-20 or more.
Results may differ from a plain program's by a relative error of at most 0.0055.
Values may be sent and summed in bfloat16 or wider, within the bound.
A program may use at most 64 MiB of HBM per device.

v0:
```python
import jax
import jax.numpy as jnp
from jax import lax
from jax.sharding import PartitionSpec as P

TILE_COLS = 128


block_rows = 32


def body(weights, owner_map):
    rows_here, cols_here = weights.shape
    tile_cols = TILE_COLS
    row_blocks = rows_here // block_rows
    col_blocks = cols_here // tile_cols
    count = row_blocks * col_blocks
    devices = lax.axis_size(("fsdp", "tp"))
    per_peer = count // devices
    local_max = jnp.max(jnp.abs(weights)).astype(jnp.float32)
    tiles = weights.reshape(row_blocks, block_rows, col_blocks, tile_cols).transpose(0, 2, 1, 3)
    tiles = tiles.reshape(count, block_rows, tile_cols)
    order = jnp.argsort(owner_map[0], stable=True)
    chosen = tiles[order].astype(jnp.float32)
    clipped = jnp.maximum(jnp.max(jnp.abs(chosen), axis=1), 1.0)
    factor = 448.0 / clipped
    quantized = (chosen * factor[:, None, :]).astype(jnp.bfloat16)
    own_peak = jnp.full((devices, 1), local_max, jnp.float32).astype(jnp.bfloat16)
    send_tiles = quantized.reshape(devices, per_peer, block_rows, tile_cols)
    send_scales = clipped.reshape(devices, per_peer, tile_cols)
    got_tiles, got_scales, got_peak = (
        lax.all_to_all(send_tiles, ("fsdp", "tp"), split_axis=0, concat_axis=0, tiled=True),
        lax.all_to_all(
            send_scales.astype(jnp.bfloat16),
            ("fsdp", "tp"),
            split_axis=0,
            concat_axis=0,
            tiled=True,
        ).astype(send_scales.dtype),
        lax.all_to_all(own_peak, ("fsdp", "tp"), split_axis=0, concat_axis=0, tiled=True),
    )
    served_tiles = got_tiles.reshape(count, block_rows, tile_cols)
    served_scales = got_scales.reshape(count, tile_cols)
    received_amax = jnp.max(got_peak.astype(jnp.float32))
    served_scales = served_scales / received_amax
    return (served_tiles, served_scales)


def solution(mesh):
    return jax.shard_map(
        body,
        mesh=mesh,
        in_specs=(P("fsdp", "tp"), P(("fsdp", "tp"), None)),
        out_specs=(P(("fsdp", "tp"), None, None), P(("fsdp", "tp"), None)),
        check_vma=False,
    )
```

profile of v0, /device:TPU:1, one launch (start us, length us, event | category | flops | bytes accessed | tf_op | source)
XLA Modules:
  0.0 81.5 jit_solution(4499525638930426815)
XLA Ops:
  0.6 0.0 copy-start
  0.6 0.0 copy-start.1
  0.6 2.6 %abs_reduce_fusion.1 = bf16[]{:T(256)} fusion(bf16[256,4096]{1,0:T(8,128)(2,1)} %param.2), kind=kLoop, calls=%fused_computation.4 | loop fusion | flops 2097151 | bytes 2097154 | tf_op jit(solution)/shard_map/reduce_max | solution.py:20
  3.3 1.3 %broadcast_in_dim.8 = bf16[128,1,1]{2,1,0:T(2,128)(2,1)} broadcast(bf16[]{:T(256)} %abs_reduce_fusion.1), dimensions={} | broadcast | bytes 258 | tf_op jit(solution)/shard_map/broadcast_in_dim | solution.py:28
  4.6 11.5 %all-to-all-start.2 = ((bf16[128,1,1]{2,1,0:T(2,128)(2,1)}), bf16[128,1,1]{2,1,0:T(2,128)(2,1)S(1)}, u32[]{:S(2)}, u32[]{:S(2)}) async-start(bf16[128,1,1]{2,1,0:T(2,128)(2,1)} %broadcast_in_dim.8), calls=%async_computation.2 | async-start | bytes 131072 | tf_op jit(solution)/shard_map/all_to_all | solution.py:40
  16.1 0.0 copy-done.1
  16.1 3.2 %sort.17 = (s32[256]{0:T(256)}, s32[256]{0:T(256)S(1)}) sort(s32[256]{0:T(256)S(1)} %bitcast.25, s32[256]{0:T(256)S(1)} %iota.4), dimensions={0}, to_apply=%region_0.0 | sort | flops 2048 | bytes 4096 | tf_op jit(solution)/shard_map/jit(argsort)/sort | solution.py:23
  19.3 0.0 copy-done
  19.3 0.5 copy.9
  19.8 0.4 bitcast_bitcast_fusion
  20.1 2.1 %copy.6 = bf16[8,32,32,128]{3,2,1,0:T(8,128)(2,1)} copy(bf16[8,32,32,128]{3,1,2,0:T(8,128)(2,1)S(1)} %bitcast_bitcast_fusion) | data formatting | bytes 4194304 | tf_op jit(solution)/shard_map/transpose | solution.py:21
  22.3 2.6 %gather_fusion = bf16[256,32,128]{2,1,0:T(8,128)(2,1)S(1)} fusion(bf16[256,32,128]{2,1,0:T(8,128)(2,1)} %bitcast.18, s32[1024]{0:T(1024)S(1)} %pad_clamp_fusion), kind=kCustom, calls=%fused_computation | custom fusion | bytes 4195328 | tf_op jit(solution)/shard_map/gather | solution.py:24
  24.9 1.1 %abs_reduce_fusion = f32[256,128]{1,0:T(8,128)S(1)} fusion(bf16[256,32,128]{2,1,0:T(8,128)(2,1)S(1)} %gather_fusion), kind=kLoop, calls=%fused_computation.2 | loop fusion | flops 3112960 | bytes 2228224 | tf_op jit(solution)/shard_map/reduce_max | solution.py:25
  26.0 0.6 maximum_convert_fusion
  26.7 0.0 all-to-all-done.2
  26.7 9.8 %all-to-all-start.1 = ((bf16[128,2,128]{2,1,0:T(2,128)(2,1)}), bf16[128,2,128]{2,1,0:T(2,128)(2,1)S(1)}, u32[]{:S(2)}, u32[]{:S(2)}) async-start(bf16[128,2,128]{2,1,0:T(2,128)(2,1)} %bitcast.6), calls=%async_computation.1 | async-start | bytes 131072 | tf_op jit(solution)/shard_map/all_to_all | solution.py:33
  36.4 2.0 %multiply_convert_fusion = bf16[128,2,32,128]{3,2,1,0:T(8,128)(2,1)} fusion(f32[128,2,128]{2,1,0:T(2,128)S(1)} %bitcast.22, bf16[128,2,32,128]{3,2,1,0:T(8,128)(2,1)S(1)} %bitcast.17), kind=kLoop, calls=%fused_computation.1 | loop fusion | flops 3145728 | bytes 4325376 | tf_op jit(solution)/shard_map/convert_element_type | solution.py:27
  38.4 7.6 %all-to-all-done.1 = bf16[128,2,128]{2,1,0:T(2,128)(2,1)S(1)} async-done(((bf16[128,2,128]{2,1,0:T(2,128)(2,1)}), bf16[128,2,128]{2,1,0:T(2,128)(2,1)S(1)}, u32[]{:S(2)}, u32[]{:S(2)}) %all-to-all-start.1) | async-done | bytes 65568 | tf_op jit(solution)/shard_map/all_to_all | solution.py:33
  46.0 4.6 %all-to-all-start = ((bf16[128,2,32,128]{3,2,1,0:T(8,128)(2,1)}), bf16[128,2,32,128]{3,2,1,0:T(8,128)(2,1)S(1)}, u32[]{:S(2)}, u32[]{:S(2)}) async-start(bf16[128,2,32,128]{3,2,1,0:T(8,128)(2,1)} %multiply_convert_fusion), calls=%async_computation | async-start | bytes 4194304 | tf_op jit(solution)/shard_map/all_to_all | solution.py:32
  50.5 0.7 reduce_max.34
  51.9 0.7 convert_divide_fusion
  52.6 27.6 %all-to-all-done = bf16[128,2,32,128]{3,2,1,0:T(8,128)(2,1)S(1)} async-done(((bf16[128,2,32,128]{3,2,1,0:T(8,128)(2,1)}), bf16[128,2,32,128]{3,2,1,0:T(8,128)(2,1)S(1)}, u32[]{:S(2)}, u32[]{:S(2)}) %all-to-all-start) | async-done | bytes 2097184 | tf_op jit(solution)/shard_map/all_to_all | solution.py:32
  80.2 1.3 %copy.11 = bf16[256,32,128]{2,1,0:T(8,128)(2,1)} copy(bf16[256,32,128]{2,1,0:T(8,128)(2,1)S(1)} %bitcast.20) | data formatting | bytes 4194304
  (4 shorter events, 0.0 us)
Async XLA Ops:
  0.6 18.6 %copy-start = (bf16[256,4096]{1,0:T(8,128)(2,1)S(1)}, bf16[256,4096]{1,0:T(8,128)(2,1)}, u32[]{:S(2)}) copy-start(bf16[256,4096]{1,0:T(8,128)(2,1)} %param.2) | copy-start | bytes 6291460
  0.6 15.4 %copy-start.1 = (s32[1,256]{1,0:T(1,128)S(1)}, s32[1,256]{1,0:T(1,128)}, u32[]{:S(2)}) copy-start(s32[1,256]{1,0:T(1,128)} %param.3) | copy-start | bytes 3076
  4.6 22.1 %all-to-all-start.2 = ((bf16[128,1,1]{2,1,0:T(2,128)(2,1)}), bf16[128,1,1]{2,1,0:T(2,128)(2,1)S(1)}, u32[]{:S(2)}, u32[]{:S(2)}) async-start(bf16[128,1,1]{2,1,0:T(2,128)(2,1)} %broadcast_in_dim.8), calls=%async_computation.2 | async-start | bytes 131072 | tf_op jit(solution)/shard_map/all_to_all | solution.py:40
  26.7 19.3 %all-to-all-start.1 = ((bf16[128,2,128]{2,1,0:T(2,128)(2,1)}), bf16[128,2,128]{2,1,0:T(2,128)(2,1)S(1)}, u32[]{:S(2)}, u32[]{:S(2)}) async-start(bf16[128,2,128]{2,1,0:T(2,128)(2,1)} %bitcast.6), calls=%async_computation.1 | async-start | bytes 131072 | tf_op jit(solution)/shard_map/all_to_all | solution.py:33
  46.0 34.2 %all-to-all-start = ((bf16[128,2,32,128]{3,2,1,0:T(8,128)(2,1)}), bf16[128,2,32,128]{3,2,1,0:T(8,128)(2,1)S(1)}, u32[]{:S(2)}, u32[]{:S(2)}) async-start(bf16[128,2,32,128]{3,2,1,0:T(8,128)(2,1)} %multiply_convert_fusion), calls=%async_computation | async-start | bytes 4194304 | tf_op jit(solution)/shard_map/all_to_all | solution.py:32
where the time goes:
time: 81.8 us; the launch traced here: 81.5 us
  waiting for transfers between devices  35.2 us (43%)
  starting transfers between devices  25.8 us (32%)
  other arithmetic  11 us (13%)
  local copies, waits for them, and re-layouts  8.19 us (10%)
  between operations  1.39 us (2%)
    all_to_all x1, waiting for transfers between devices, body(): lax.all_to_all(send_tiles, ('fsdp', 'tp'), split_axis=0, concat_axis=0, t...  27.6 us
    all_to_all x1, starting transfers between devices, body(): lax.all_to_all(own_peak, ('fsdp', 'tp'), split_axis=0, concat_axis=0, til...  11.5 us
    all_to_all x1, starting transfers between devices, body(): lax.all_to_all(send_scales.astype(jnp.bfloat16), ('fsdp', 'tp'), split_ax...  9.76 us
    all_to_all x1, waiting for transfers between devices, body(): lax.all_to_all(send_scales.astype(jnp.bfloat16), ('fsdp', 'tp'), split_ax...  7.57 us
    all_to_all x1, starting transfers between devices, body(): lax.all_to_all(send_tiles, ('fsdp', 'tp'), split_axis=0, concat_axis=0, t...  4.58 us
    sort x1, other arithmetic, body(): order = jnp.argsort(owner_map[0], stable=True)  3.17 us
    reduce_max x1, other arithmetic, body(): local_max = jnp.max(jnp.abs(weights)).astype(jnp.float32)  2.63 us
    gather x1, local copies, waits for them, and re-layouts, body(): chosen = tiles[order].astype(jnp.float32)  2.58 us
  transfers between devices with their start and end apart: 3, of which 2 were waited for; matrix products, arithmetic and copies ran while one was open for 17% of the time, Pallas kernels for 0%

commit v1 on v0

v1 whole, which is shorter than its diff:
```python
import random

import jax
import jax.numpy as jnp
from jax import lax
from jax.experimental import pallas as pl
from jax.experimental.pallas import tpu as pltpu
from jax.sharding import PartitionSpec as P

MESH = pl.DeviceIdType.MESH
N = 128
TILES = 256
ROWS = 32
LANES = 128
BLOCKS = 32
F32 = jnp.float32
BF16 = jnp.bfloat16
I32 = jnp.int32


def _hops(m):
    ring = (0, 1, 2, 1)
    return ring[(m >> 2) & 3] + ring[(m >> 4) & 3] + ring[(m >> 6) * 2 + ((m >> 1) & 1)]


def _plane(m):
    return (m >> 6) == 0 and ((m >> 1) & 1) == 0


PRE = 40
_rng = random.Random(3)
_all = list(range(1, N))
_rng.shuffle(_all)
_all.sort(key=lambda m: -_hops(m))
NEAR = [m for m in _all if _hops(m) <= 3 or _plane(m)]
_first = [m for m in _all if _hops(m) == 3][:PRE]
ORDER = _first + [m for m in _all if m not in _first] + [0]
LINE_Z = [2, 64, 66]
LINE_Y = [16, 32, 48]
LINE_X = [1, 4, 5, 8, 9, 12, 13]
CUTS = list(range(0, 120, 8)) + [120, 124, 127]
LINES = len(LINE_X) + len(LINE_Y) + len(LINE_Z)


def _dev(p):
    return (lax.div(p, 4), lax.rem(p, 4))


def _body(w_hbm, map_hbm, out_ref, scale_ref, wv, sbuf, rbuf, table, map_s, pos_v, pos_s,
          peak_out, peak_in, copy_sem, map_sem, pos_sem, send_sem, recv_sem, peak_send, peak_recv, all_sem):
    me = lax.axis_index("fsdp") * 4 + lax.axis_index("tp")
    barrier = pltpu.get_barrier_semaphore()

    def partner(m):
        return jnp.bitwise_xor(me, m)

    map_copy = pltpu.make_async_copy(map_hbm, map_s, map_sem)
    map_copy.start()
    for m in NEAR:
        pl.semaphore_signal(barrier, inc=1, device_id=_dev(partner(m)), device_id_type=MESH)
    w_copies = []
    for c in range(BLOCKS):
        w_copies.append(pltpu.make_async_copy(
            w_hbm.at[:, :, pl.ds(c * LANES, LANES)], wv.at[pl.ds(c * 8, 8)], copy_sem))
        w_copies[-1].start()

    for k, m in enumerate(ORDER):
        table[k] = m

    map_copy.wait()
    lane = lax.broadcasted_iota(I32, (8, LANES), 1)

    def slot(j):
        return lax.rem(j, BLOCKS) * 8 + lax.div(j, BLOCKS)

    def find(i, pos):
        low, high = pos
        for u in range(8):
            up = i * 8 + u
            down = TILES - 1 - up
            high = jnp.where(lane == map_s[0, up], slot(up), high)
            low = jnp.where(lane == map_s[0, down], slot(down), low)
        return low, high

    zero = jnp.zeros((8, LANES), I32)
    low, high = lax.fori_loop(0, TILES // 8, find, (zero, zero))
    pos_v[0] = low
    pos_v[1] = high
    pos_copy = pltpu.make_async_copy(pos_v, pos_s, pos_sem)
    pos_copy.start()

    pltpu.make_async_copy(wv, wv, copy_sem).wait()

    def largest(i, acc):
        x = jnp.abs(wv[pl.ds(i * 8, 8)])
        return jnp.maximum(acc, jnp.max(x.reshape(16, 16, LANES), axis=0))

    peak = lax.fori_loop(0, BLOCKS, largest, jnp.zeros((16, LANES), BF16)).astype(F32)
    peak = jnp.maximum(peak[:8], peak[8:])
    peak_out[0] = peak

    pos_copy.wait()

    def gather(i, _):
        for u in range(4):
            d = i * 4 + u
            for h in range(2):
                sbuf[d, h] = wv[pos_s[h, 0, d]]
        return 0

    lax.fori_loop(0, N // 4, gather, 0)

    def message(k, p, group):
        return pltpu.make_async_remote_copy(
            src_ref=sbuf.at[p], dst_ref=rbuf.at[k], send_sem=send_sem, recv_sem=recv_sem.at[group],
            device_id=_dev(p), device_id_type=MESH)

    def send(group):
        def one(k, _):
            message(k, partner(table[k]), group).start()
            return 0

        lax.fori_loop(CUTS[group], CUTS[group + 1], one, 0)

    def arrivals(group):
        span = pl.ds(CUTS[group], CUTS[group + 1] - CUTS[group])
        return pltpu.make_async_remote_copy(
            src_ref=sbuf.at[span], dst_ref=rbuf.at[span], send_sem=send_sem, recv_sem=recv_sem.at[group],
            device_id=_dev(me), device_id_type=MESH)

    def peaks(stage, line, base):
        copies = [pltpu.make_async_remote_copy(
            src_ref=peak_out.at[stage], dst_ref=peak_in.at[base + i],
            send_sem=peak_send, recv_sem=peak_recv.at[stage],
            device_id=_dev(partner(m)), device_id_type=MESH) for i, m in enumerate(line)]
        for c in copies:
            c.start()

    def fold(stage, line, base, value):
        span = pl.ds(base, len(line))
        pltpu.make_async_remote_copy(
            src_ref=peak_in.at[span], dst_ref=peak_in.at[span], send_sem=peak_send, recv_sem=peak_recv.at[stage],
            device_id=_dev(me), device_id_type=MESH).wait_recv()
        for i in range(len(line)):
            value = jnp.maximum(value, peak_in[base + i])
        return value

    def finish(p, pair):
        x = pair.astype(F32)
        clipped = jnp.maximum(jnp.max(jnp.abs(x), axis=1, keepdims=True), 1.0)
        out_ref[pl.ds(2 * p, 2)] = (x * (448.0 / clipped)).astype(BF16)
        scale_ref[pl.ds(2 * p, 2), :] = clipped.reshape(2, LANES)

    def receive(group):
        arrivals(group).wait_recv()

        def one(k, _):
            finish(partner(table[k]), rbuf[k])
            return 0

        lax.fori_loop(CUTS[group], CUTS[group + 1], one, 0)

    pl.semaphore_wait(barrier, len(NEAR))
    for m in LINE_Z:
        pl.semaphore_signal(all_sem, inc=1, device_id=_dev(partner(m)), device_id_type=MESH)
    peaks(0, LINE_X, 0)
    for g in range(PRE // 8):
        send(g)
    pl.semaphore_wait(all_sem, len(LINE_Z))
    half = max(PRE // 8, 6)
    for g in range(PRE // 8, half):
        send(g)
    peak = fold(0, LINE_X, 0, peak)
    peak_out[1] = peak
    finish(me, sbuf[me])
    peaks(1, LINE_Y, len(LINE_X))
    for g in range(half, 11):
        send(g)
    for g in range(2):
        receive(g)
    peak = fold(1, LINE_Y, len(LINE_X), peak)
    peak_out[2] = peak
    receive(2)
    peaks(2, LINE_Z, len(LINE_X) + len(LINE_Y))
    for g in range(11, len(CUTS) - 1):
        send(g)
    for g in range(3, 12):
        receive(g)
    peak = fold(2, LINE_Z, len(LINE_X) + len(LINE_Y), peak)
    top = jnp.max(peak, keepdims=True)
    for g in range(12, len(CUTS) - 1):
        receive(g)
    scale_ref[...] = scale_ref[...] / top
    every = pl.ds(0, N - 1)
    pltpu.make_async_remote_copy(
        src_ref=sbuf.at[every], dst_ref=rbuf.at[every], send_sem=send_sem, recv_sem=recv_sem.at[0],
        device_id=_dev(me), device_id_type=MESH).wait_send()
    every = pl.ds(0, LINES)
    pltpu.make_async_remote_copy(
        src_ref=peak_in.at[every], dst_ref=peak_in.at[every], send_sem=peak_send, recv_sem=recv_sem.at[0],
        device_id=_dev(me), device_id_type=MESH).wait_send()


def _exchange(weights, owner_map):
    hbm = pl.BlockSpec(memory_space=pltpu.HBM)
    vmem = pl.BlockSpec(memory_space=pltpu.VMEM)
    return pl.pallas_call(
        _body,
        name="exchange",
        out_shape=(jax.ShapeDtypeStruct((TILES, ROWS, LANES), BF16), jax.ShapeDtypeStruct((TILES, LANES), F32)),
        in_specs=[hbm, hbm],
        out_specs=(vmem, vmem),
        scratch_shapes=[
            pltpu.VMEM((TILES, ROWS, LANES), BF16),
            pltpu.VMEM((N, 2, ROWS, LANES), BF16),
            pltpu.VMEM((N, 2, ROWS, LANES), BF16),
            pltpu.SMEM((N,), I32),
            pltpu.SMEM((1, TILES), I32),
            pltpu.VMEM((2, 8, LANES), I32),
            pltpu.SMEM((2, 8, LANES), I32),
            pltpu.VMEM((3, 8, LANES), F32),
            pltpu.VMEM((LINES, 8, LANES), F32),
            pltpu.SemaphoreType.DMA,
            pltpu.SemaphoreType.DMA,
            pltpu.SemaphoreType.DMA,
            pltpu.SemaphoreType.DMA,
            pltpu.SemaphoreType.DMA((len(CUTS) - 1,)),
            pltpu.SemaphoreType.DMA,
            pltpu.SemaphoreType.DMA((3,)),
            pltpu.SemaphoreType.REGULAR,
        ],
        compiler_params=pltpu.CompilerParams(
            collective_id=0, has_side_effects=True, vmem_limit_bytes=24 * 2**20),
    )(pltpu.with_memory_space_constraint(weights.reshape(8, ROWS, -1), pltpu.HBM), pltpu.with_memory_space_constraint(owner_map, pltpu.HBM))


def _flush_body(tiles_ref, scales_ref, out_ref, scale_ref, sem):
    copies = [pltpu.make_async_copy(scales_ref, scale_ref, sem.at[8])]
    step = TILES // 8
    for i in range(8):
        copies.append(pltpu.make_async_copy(
            tiles_ref.at[pl.ds(i * step, step)], out_ref.at[pl.ds(i * step, step)], sem.at[i]))
    for c in copies:
        c.start()
    for c in copies:
        c.wait()


def _flush(tiles, scales):
    hbm = pl.BlockSpec(memory_space=pltpu.HBM)
    vmem = pl.BlockSpec(memory_space=pltpu.VMEM)
    return pl.pallas_call(
        _flush_body,
        name="flush",
        out_shape=(jax.ShapeDtypeStruct((TILES, ROWS, LANES), BF16), jax.ShapeDtypeStruct((TILES, LANES), F32)),
        in_specs=[vmem, vmem],
        out_specs=(hbm, hbm),
        scratch_shapes=[pltpu.SemaphoreType.DMA((9,))],
        compiler_params=pltpu.CompilerParams(vmem_limit_bytes=16 * 2**20),
    )(tiles, scales)


def body(weights, owner_map):
    return _flush(*_exchange(weights, owner_map))


def solution(mesh):
    return jax.shard_map(
        body,
        mesh=mesh,
        in_specs=(P("fsdp", "tp"), P(("fsdp", "tp"), None)),
        out_specs=(P(("fsdp", "tp"), None, None), P(("fsdp", "tp"), None)),
        check_vma=False,
    )
```

time: 81.8 us -> 39.2 us (0.48)
  Pallas kernels: 0 us -> 38.4 us
  waiting for transfers between devices: 35.2 us -> 0 us
  starting transfers between devices: 25.8 us -> 0 us
  other arithmetic: 11 us -> 0 us
  local copies, waits for them, and re-layouts: 8.19 us -> 0 us
    pallas_call x0 -> x2, Pallas kernels: none -> 38.4 us  [the longest x1 37 us: _exchange(): pl.pallas_call(_body, name='exchange', out_shape=(jax.ShapeDtypeStruct((T...]
    all_to_all x3 -> x0, waiting for transfers between devices: 35.2 us -> none  [the longest x1 27.6 us: body(): lax.all_to_all(send_tiles, ('fsdp', 'tp'), split_axis=0, concat_axis=0, t...]
    all_to_all x3 -> x0, starting transfers between devices: 25.8 us -> none  [the longest x1 11.5 us: body(): lax.all_to_all(own_peak, ('fsdp', 'tp'), split_axis=0, concat_axis=0, til...]
    reduce_max x3 -> x0, other arithmetic: 4.49 us -> none  [the longest x1 2.63 us: body(): local_max = jnp.max(jnp.abs(weights)).astype(jnp.float32)]
    sort x1 -> x0, other arithmetic: 3.17 us -> none  [body(): order = jnp.argsort(owner_map[0], stable=True)]
    convert_element_type x2 -> x0, other arithmetic: 2.6 us -> none  [the longest x1 1.96 us: body(): quantized = (chosen * factor[:, None, :]).astype(jnp.bfloat16)]
    gather x1 -> x0, local copies, waits for them, and re-layouts: 2.58 us -> none  [body(): chosen = tiles[order].astype(jnp.float32)]
    transpose x2 -> x0, local copies, waits for them, and re-layouts: 2.5 us -> none  [body(): weights.reshape(row_blocks, block_rows, col_blocks, tile_cols)]
  transfers between devices with their start and end apart: 3 -> 0, of which waited for: 2 -> 0; matrix products, arithmetic and copies ran while one was open for 17% -> 0% of each run, Pallas kernels for 0% -> 0%
where the time goes in v1:
time: 39.2 us; the launch traced here: 39.1 us
  Pallas kernels  38.4 us (98%)
  between operations  0.64 us (2%)
    pallas_call x1, Pallas kernels, _exchange(): pl.pallas_call(_body, name='exchange', out_shape=(jax.ShapeDtypeStruct((T...  37 us
    pallas_call x1, Pallas kernels, _flush(): pl.pallas_call(_flush_body, name='flush', out_shape=(jax.ShapeDtypeStruct...  1.43 us

profile of v1, /device:TPU:1, one launch (start us, length us, event | category | flops | bytes accessed | tf_op | source)
XLA Modules:
  0.0 39.1 jit_solution(1765764282501754845)
XLA Ops:
  0.6 37.0 %exchange.1 = (bf16[256,32,128]{2,1,0:T(8,128)(2,1)S(1)}, f32[256,128]{1,0:T(8,128)S(1)}) custom-call(bf16[8,32,4096]{2,1,0:T(8,128)(2,1)} %bitcast.1, s32[1,256]{1,0:T(1,128)} %map_hbm.1), custom_call_target="tpu_custom_call" | custom-call | tf_op jit(solution)/shard_map/exchange/pallas_call | solution.py:207
  37.6 1.4 %flush.1 = (bf16[256,32,128]{2,1,0:T(8,128)(2,1)}, f32[256,128]{1,0:T(8,128)}) custom-call(bf16[256,32,128]{2,1,0:T(8,128)(2,1)S(1)} %get-tuple-element.4.tiles_ref, f32[256,128]{1,0:T(8,128)S(1)} %get-tuple-element.5.scales_ref), custom_call_target="tpu_custom_call" | custom-call | tf_op jit(solution)/shard_map/flush/pallas_call | solution.py:252

commit v2 on v1

--- a/solution.py
+++ b/solution.py
@@ -27,14 +27,26 @@
     return (m >> 6) == 0 and ((m >> 1) & 1) == 0
 
 
+PRE_CORE = 16
 PRE = 40
 _rng = random.Random(3)
 _all = list(range(1, N))
 _rng.shuffle(_all)
 _all.sort(key=lambda m: -_hops(m))
-NEAR = [m for m in _all if _hops(m) <= 3 or _plane(m)]
-_first = [m for m in _all if _hops(m) == 3][:PRE]
-ORDER = _first + [m for m in _all if m not in _first] + [0]
+NEAR = [m for m in _all if (m % 2 == 0 and (_hops(m) <= 3 or _plane(m))) or m == 1]
+ORDER = [
+    74, 34, 44, 66, 62, 118, 86, 80, 30, 36, 54, 24, 126, 22, 112, 98,
+    11, 45, 113, 37, 63, 31, 69, 95, 119, 55, 35, 87, 75, 77, 127, 94,
+    57, 99, 76, 68, 23, 25, 81, 10, 120, 106, 121, 89, 101, 109, 100, 108,
+    105, 42, 107, 88, 43, 26, 92, 103, 117, 47, 116, 93, 67, 90, 96, 27,
+    59, 111, 72, 84, 85, 97, 91, 124, 110, 125, 46, 58, 122, 123, 39, 102,
+    71, 52, 7, 60, 21, 40, 19, 14, 73, 104, 9, 61, 79, 20, 82, 78,
+    65, 50, 64, 51, 8, 6, 83, 15, 32, 18, 114, 5, 70, 115, 33, 28,
+    29, 13, 3, 49, 53, 41, 12, 16, 17, 56, 48, 4, 2, 1, 38,
+]
+assert sorted(ORDER) == list(range(1, N))
+assert all(m in NEAR and m > 1 for m in ORDER[:PRE_CORE])
+assert all(m in NEAR or m - 1 in NEAR for m in ORDER[:PRE] if m > 1)
 LINE_Z = [2, 64, 66]
 LINE_Y = [16, 32, 48]
 LINE_X = [1, 4, 5, 8, 9, 12, 13]
@@ -47,23 +59,26 @@
 
 
 def _body(w_hbm, map_hbm, out_ref, scale_ref, wv, sbuf, rbuf, table, map_s, pos_v, pos_s,
-          peak_out, peak_in, copy_sem, map_sem, pos_sem, send_sem, recv_sem, peak_send, peak_recv, all_sem):
+          peak_out, peak_in, copy_sem, map_sem, pos_sem, send_sem, recv_sem, peak_send, peak_recv, all_sem, pair_sem):
     me = lax.axis_index("fsdp") * 4 + lax.axis_index("tp")
     barrier = pltpu.get_barrier_semaphore()
 
     def partner(m):
         return jnp.bitwise_xor(me, m)
 
+    def tell(sem, m):
+        pl.semaphore_signal(sem, inc=1, device_id=_dev(partner(m)), device_id_type=MESH)
+
     map_copy = pltpu.make_async_copy(map_hbm, map_s, map_sem)
     map_copy.start()
-    for m in NEAR:
-        pl.semaphore_signal(barrier, inc=1, device_id=_dev(partner(m)), device_id_type=MESH)
     w_copies = []
     for c in range(BLOCKS):
         w_copies.append(pltpu.make_async_copy(
             w_hbm.at[:, :, pl.ds(c * LANES, LANES)], wv.at[pl.ds(c * 8, 8)], copy_sem))
         w_copies[-1].start()
 
+    for m in NEAR:
+        tell(barrier, m)
     for k, m in enumerate(ORDER):
         table[k] = m
 
@@ -84,28 +99,20 @@
 
     zero = jnp.zeros((8, LANES), I32)
     low, high = lax.fori_loop(0, TILES // 8, find, (zero, zero))
-    pos_v[0] = low
-    pos_v[1] = high
-    pos_copy = pltpu.make_async_copy(pos_v, pos_s, pos_sem)
+    pos_v[0:1, :] = low[0:1]
+    pos_v[1:2, :] = high[0:1]
+    both = pl.ds(0, 2)
+    pos_copy = pltpu.make_async_copy(pos_v.at[both], pos_s.at[both], pos_sem)
     pos_copy.start()
 
     pltpu.make_async_copy(wv, wv, copy_sem).wait()
-
-    def largest(i, acc):
-        x = jnp.abs(wv[pl.ds(i * 8, 8)])
-        return jnp.maximum(acc, jnp.max(x.reshape(16, 16, LANES), axis=0))
-
-    peak = lax.fori_loop(0, BLOCKS, largest, jnp.zeros((16, LANES), BF16)).astype(F32)
-    peak = jnp.maximum(peak[:8], peak[8:])
-    peak_out[0] = peak
-
     pos_copy.wait()
 
     def gather(i, _):
         for u in range(4):
             d = i * 4 + u
             for h in range(2):
-                sbuf[d, h] = wv[pos_s[h, 0, d]]
+                sbuf[d, h] = wv[pos_s[h, d]]
         return 0
 
     lax.fori_loop(0, N // 4, gather, 0)
@@ -162,11 +169,30 @@
 
     pl.semaphore_wait(barrier, len(NEAR))
     for m in LINE_Z:
-        pl.semaphore_signal(all_sem, inc=1, device_id=_dev(partner(m)), device_id_type=MESH)
+        tell(all_sem, m)
+    tell(pair_sem.at[0], 1)
+    for g in range(PRE_CORE // 8):
+        send(g)
+
+    def largest(i, ends):
+        high, low = ends
+        for u in range(8):
+            x = wv[i * 8 + u]
+            high, low = jnp.maximum(high, x), jnp.minimum(low, x)
+        return high, low
+
+    zero = jnp.zeros((ROWS, LANES), BF16)
+    high, low = lax.fori_loop(0, BLOCKS, largest, (zero, zero))
+    peak = jnp.maximum(high.astype(F32), -low.astype(F32))
+    peak = jnp.maximum(jnp.maximum(peak[:8], peak[8:16]), jnp.maximum(peak[16:24], peak[24:]))
+    peak_out[0] = peak
+    pl.semaphore_wait(pair_sem.at[0], 1)
     peaks(0, LINE_X, 0)
-    for g in range(PRE // 8):
+    for g in range(PRE_CORE // 8, PRE // 8):
         send(g)
     pl.semaphore_wait(all_sem, len(LINE_Z))
+    tell(pair_sem.at[1], 1)
+    pl.semaphore_wait(pair_sem.at[1], 1)
     half = max(PRE // 8, 6)
     for g in range(PRE // 8, half):
         send(g)
@@ -216,8 +242,8 @@
             pltpu.VMEM((N, 2, ROWS, LANES), BF16),
             pltpu.SMEM((N,), I32),
             pltpu.SMEM((1, TILES), I32),
-            pltpu.VMEM((2, 8, LANES), I32),
-            pltpu.SMEM((2, 8, LANES), I32),
+            pltpu.VMEM((8, LANES), I32),
+            pltpu.SMEM((8, LANES), I32),
             pltpu.VMEM((3, 8, LANES), F32),
             pltpu.VMEM((LINES, 8, LANES), F32),
             pltpu.SemaphoreType.DMA,
@@ -228,6 +254,7 @@
             pltpu.SemaphoreType.DMA,
             pltpu.SemaphoreType.DMA((3,)),
             pltpu.SemaphoreType.REGULAR,
+            pltpu.SemaphoreType.REGULAR((2,)),
         ],
         compiler_params=pltpu.CompilerParams(
             collective_id=0, has_side_effects=True, vmem_limit_bytes=24 * 2**20),
@@ -235,9 +262,9 @@
 
 
 def _flush_body(tiles_ref, scales_ref, out_ref, scale_ref, sem):
-    copies = [pltpu.make_async_copy(scales_ref, scale_ref, sem.at[8])]
-    step = TILES // 8
-    for i in range(8):
+    copies = [pltpu.make_async_copy(scales_ref, scale_ref, sem.at[2])]
+    step = TILES // 2
+    for i in range(2):
         copies.append(pltpu.make_async_copy(
             tiles_ref.at[pl.ds(i * step, step)], out_ref.at[pl.ds(i * step, step)], sem.at[i]))
     for c in copies:
@@ -255,7 +282,7 @@
         out_shape=(jax.ShapeDtypeStruct((TILES, ROWS, LANES), BF16), jax.ShapeDtypeStruct((TILES, LANES), F32)),
         in_specs=[vmem, vmem],
         out_specs=(hbm, hbm),
-        scratch_shapes=[pltpu.SemaphoreType.DMA((9,))],
+        scratch_shapes=[pltpu.SemaphoreType.DMA((3,))],
         compiler_params=pltpu.CompilerParams(vmem_limit_bytes=16 * 2**20),
     )(tiles, scales)
 

time: 39.2 us -> 38.4 us (0.980)
  Pallas kernels: 38.4 us -> 37.3 us
    pallas_call x1, Pallas kernels: 37 us -> 35.9 us  [_exchange(): pl.pallas_call(_body, name='exchange', out_shape=(jax.ShapeDtypeStruct((T...]
where the time goes in v2:
time: 38.4 us; the launch traced here: 37.9 us
  Pallas kernels  37.3 us (97%)
  between operations  0.64 us (2%)
    pallas_call x1, Pallas kernels, _exchange(): pl.pallas_call(_body, name='exchange', out_shape=(jax.ShapeDtypeStruct((T...  35.9 us
    pallas_call x1, Pallas kernels, _flush(): pl.pallas_call(_flush_body, name='flush', out_shape=(jax.ShapeDtypeStruct...  1.39 us

profile of v2, /device:TPU:1, one launch (start us, length us, event | category | flops | bytes accessed | tf_op | source)
XLA Modules:
  0.0 37.9 jit_solution(566932615831050475)
XLA Ops:
  0.6 35.9 %exchange.1 = (bf16[256,32,128]{2,1,0:T(8,128)(2,1)S(1)}, f32[256,128]{1,0:T(8,128)S(1)}) custom-call(bf16[8,32,4096]{2,1,0:T(8,128)(2,1)} %bitcast.1, s32[1,256]{1,0:T(1,128)} %map_hbm.1), custom_call_target="tpu_custom_call" | custom-call | tf_op jit(solution)/shard_map/exchange/pallas_call | solution.py:233
  36.5 1.4 %flush.1 = (bf16[256,32,128]{2,1,0:T(8,128)(2,1)}, f32[256,128]{1,0:T(8,128)}) custom-call(bf16[256,32,128]{2,1,0:T(8,128)(2,1)S(1)} %get-tuple-element.4.tiles_ref, f32[256,128]{1,0:T(8,128)S(1)} %get-tuple-element.5.scales_ref), custom_call_target="tpu_custom_call" | custom-call | tf_op jit(solution)/shard_map/flush/pallas_call | solution.py:279

commit v3 on v2

--- a/solution.py
+++ b/solution.py
@@ -36,13 +36,13 @@
 NEAR = [m for m in _all if (m % 2 == 0 and (_hops(m) <= 3 or _plane(m))) or m == 1]
 ORDER = [
     74, 34, 44, 66, 62, 118, 86, 80, 30, 36, 54, 24, 126, 22, 112, 98,
-    11, 45, 113, 37, 63, 31, 69, 95, 119, 55, 35, 87, 75, 77, 127, 94,
-    57, 99, 76, 68, 23, 25, 81, 10, 120, 106, 121, 89, 101, 109, 100, 108,
-    105, 42, 107, 88, 43, 26, 92, 103, 117, 47, 116, 93, 67, 90, 96, 27,
-    59, 111, 72, 84, 85, 97, 91, 124, 110, 125, 46, 58, 122, 123, 39, 102,
-    71, 52, 7, 60, 21, 40, 19, 14, 73, 104, 9, 61, 79, 20, 82, 78,
-    65, 50, 64, 51, 8, 6, 83, 15, 32, 18, 114, 5, 70, 115, 33, 28,
-    29, 13, 3, 49, 53, 41, 12, 16, 17, 56, 48, 4, 2, 1, 38,
+    23, 11, 45, 113, 37, 63, 31, 69, 95, 119, 55, 35, 87, 75, 77, 127,
+    79, 57, 99, 76, 68, 25, 81, 10, 120, 106, 121, 89, 101, 109, 100, 108,
+    105, 42, 107, 88, 43, 26, 53, 103, 123, 117, 47, 116, 93, 41, 90, 96,
+    27, 59, 111, 72, 65, 85, 97, 91, 124, 125, 46, 58, 9, 39, 102, 70,
+    52, 7, 60, 21, 40, 19, 14, 73, 110, 104, 122, 61, 94, 20, 82, 78,
+    84, 50, 64, 51, 8, 6, 83, 15, 32, 18, 114, 92, 71, 115, 33, 28,
+    29, 13, 3, 49, 5, 67, 12, 16, 17, 56, 48, 4, 2, 1, 38,
 ]
 assert sorted(ORDER) == list(range(1, N))
 assert all(m in NEAR and m > 1 for m in ORDER[:PRE_CORE])

time: 38.4 us -> 38 us (0.990)
  no operation moved by 1% of the time
where the time goes in v3:
time: 38 us; the launch traced here: 37.7 us
  Pallas kernels  37 us (97%)
  between operations  0.64 us (2%)
    pallas_call x1, Pallas kernels, _exchange(): pl.pallas_call(_body, name='exchange', out_shape=(jax.ShapeDtypeStruct((T...  35.6 us
    pallas_call x1, Pallas kernels, _flush(): pl.pallas_call(_flush_body, name='flush', out_shape=(jax.ShapeDtypeStruct...  1.39 us

profile of v3, /device:TPU:1, one launch (start us, length us, event | category | flops | bytes accessed | tf_op | source)
XLA Modules:
  0.0 37.7 jit_solution(6400412278530990856)
XLA Ops:
  0.6 35.6 %exchange.1 = (bf16[256,32,128]{2,1,0:T(8,128)(2,1)S(1)}, f32[256,128]{1,0:T(8,128)S(1)}) custom-call(bf16[8,32,4096]{2,1,0:T(8,128)(2,1)} %bitcast.1, s32[1,256]{1,0:T(1,128)} %map_hbm.1), custom_call_target="tpu_custom_call" | custom-call | tf_op jit(solution)/shard_map/exchange/pallas_call | solution.py:233
  36.3 1.4 %flush.1 = (bf16[256,32,128]{2,1,0:T(8,128)(2,1)}, f32[256,128]{1,0:T(8,128)}) custom-call(bf16[256,32,128]{2,1,0:T(8,128)(2,1)S(1)} %get-tuple-element.4.tiles_ref, f32[256,128]{1,0:T(8,128)S(1)} %get-tuple-element.5.scales_ref), custom_call_target="tpu_custom_call" | custom-call | tf_op jit(solution)/shard_map/flush/pallas_call | solution.py:279

commit v4 on v3

--- a/solution.py
+++ b/solution.py
@@ -35,14 +35,14 @@
 _all.sort(key=lambda m: -_hops(m))
 NEAR = [m for m in _all if (m % 2 == 0 and (_hops(m) <= 3 or _plane(m))) or m == 1]
 ORDER = [
-    74, 34, 44, 66, 62, 118, 86, 80, 30, 36, 54, 24, 126, 22, 112, 98,
+    74, 34, 44, 66, 62, 118, 86, 24, 80, 30, 36, 54, 126, 22, 112, 98,
     23, 11, 45, 113, 37, 63, 31, 69, 95, 119, 55, 35, 87, 75, 77, 127,
     79, 57, 99, 76, 68, 25, 81, 10, 120, 106, 121, 89, 101, 109, 100, 108,
     105, 42, 107, 88, 43, 26, 53, 103, 123, 117, 47, 116, 93, 41, 90, 96,
-    27, 59, 111, 72, 65, 85, 97, 91, 124, 125, 46, 58, 9, 39, 102, 70,
-    52, 7, 60, 21, 40, 19, 14, 73, 110, 104, 122, 61, 94, 20, 82, 78,
-    84, 50, 64, 51, 8, 6, 83, 15, 32, 18, 114, 92, 71, 115, 33, 28,
-    29, 13, 3, 49, 5, 67, 12, 16, 17, 56, 48, 4, 2, 1, 38,
+    27, 59, 111, 72, 65, 85, 97, 91, 124, 125, 46, 58, 122, 39, 102, 70,
+    52, 7, 60, 21, 17, 19, 14, 73, 110, 104, 9, 61, 94, 20, 82, 78,
+    84, 50, 64, 51, 8, 6, 83, 15, 12, 18, 114, 92, 71, 115, 33, 28,
+    29, 13, 3, 49, 5, 67, 32, 16, 40, 56, 48, 4, 2, 1, 38,
 ]
 assert sorted(ORDER) == list(range(1, N))
 assert all(m in NEAR and m > 1 for m in ORDER[:PRE_CORE])
@@ -262,11 +262,10 @@
 
 
 def _flush_body(tiles_ref, scales_ref, out_ref, scale_ref, sem):
-    copies = [pltpu.make_async_copy(scales_ref, scale_ref, sem.at[2])]
-    step = TILES // 2
-    for i in range(2):
-        copies.append(pltpu.make_async_copy(
-            tiles_ref.at[pl.ds(i * step, step)], out_ref.at[pl.ds(i * step, step)], sem.at[i]))
+    copies = [
+        pltpu.make_async_copy(tiles_ref, out_ref, sem.at[0]),
+        pltpu.make_async_copy(scales_ref, scale_ref, sem.at[1]),
+    ]
     for c in copies:
         c.start()
     for c in copies:
@@ -282,7 +281,7 @@
         out_shape=(jax.ShapeDtypeStruct((TILES, ROWS, LANES), BF16), jax.ShapeDtypeStruct((TILES, LANES), F32)),
         in_specs=[vmem, vmem],
         out_specs=(hbm, hbm),
-        scratch_shapes=[pltpu.SemaphoreType.DMA((3,))],
+        scratch_shapes=[pltpu.SemaphoreType.DMA((2,))],
         compiler_params=pltpu.CompilerParams(vmem_limit_bytes=16 * 2**20),
     )(tiles, scales)
 

time: 38 us -> 40.4 us (1.063)
  Pallas kernels: 37 us -> 39.6 us
    pallas_call x1, Pallas kernels: 35.6 us -> 38.2 us  [_exchange(): pl.pallas_call(_body, name='exchange', out_shape=(jax.ShapeDtypeStruct((T...]
where the time goes in v4:
time: 40.4 us; the launch traced here: 40.2 us
  Pallas kernels  39.6 us (98%)
  between operations  0.64 us (2%)
    pallas_call x1, Pallas kernels, _exchange(): pl.pallas_call(_body, name='exchange', out_shape=(jax.ShapeDtypeStruct((T...  38.2 us
    pallas_call x1, Pallas kernels, _flush(): pl.pallas_call(_flush_body, name='flush', out_shape=(jax.ShapeDtypeStruct...  1.36 us

profile of v4, /device:TPU:1, one launch (start us, length us, event | category | flops | bytes accessed | tf_op | source)
XLA Modules:
  0.0 40.2 jit_solution(10180826964144849619)
XLA Ops:
  0.6 38.2 %exchange.1 = (bf16[256,32,128]{2,1,0:T(8,128)(2,1)S(1)}, f32[256,128]{1,0:T(8,128)S(1)}) custom-call(bf16[8,32,4096]{2,1,0:T(8,128)(2,1)} %bitcast.1, s32[1,256]{1,0:T(1,128)} %map_hbm.1), custom_call_target="tpu_custom_call" | custom-call | tf_op jit(solution)/shard_map/exchange/pallas_call | solution.py:233
  38.9 1.4 %flush.1 = (bf16[256,32,128]{2,1,0:T(8,128)(2,1)}, f32[256,128]{1,0:T(8,128)}) custom-call(bf16[256,32,128]{2,1,0:T(8,128)(2,1)S(1)} %get-tuple-element.4.tiles_ref, f32[256,128]{1,0:T(8,128)S(1)} %get-tuple-element.5.scales_ref), custom_call_target="tpu_custom_call" | custom-call | tf_op jit(solution)/shard_map/flush/pallas_call | solution.py:278
